TPU v7x, 32 devices: a whole 2x2x4 slice. The times are simulated.
32 devices in a mesh: sky: 8 (over z, y), band: 4 (over x, core).
Axes of the slice: x: 2, y: 2, z: 4, core: 2. Of those that a mesh axis runs over, the one named last changes fastest.
Arguments:
- magnitudes: float32 [4, 8, 16384], P('band', None, 'sky'), may hold values from -7 to 7
- weights: float32 [4, 8, 16384], P('band', None, 'sky'), may hold values from 0.25 to 4
- slots: int32 [4, 8, 16384], P('band', None, 'sky'), may hold values from 0 to 31, as said below
- block_fields: int32 [64, 32], P('sky'), may hold values from 0 to 4096, as said below
- owner: int32 [4096], replicated, may hold values from 0 to 7, as said below
- colors: int32 [4096], replicated, may hold values from 0 to 7
- color_terms: float32 [4, 4], replicated, may hold values from -0.25 to 0.25
Outputs:
- zero_points: float32 [4, 4096], P('band', 'sky')
- star_mags: float32 [4, 16384], P('band', 'sky')
- misfit: float32 [4, 4], P(None, 'band')
Inputs may be any that keep to these rules, and one draw needn't show every extreme that they name: `block_fields`: the live entries of each list come first, are distinct, and name fields owned by the block's own sky tile or by the tiles one index below or above it, cyclically over 8 tiles; the remaining entries equal 4096. A list holds 16 or more live entries, and every tile has a block with all 32 live. `owner`: each sky tile owns exactly 512 fields. `slots`: each observation names a live entry of its block's list.
All inputs are finite; a program needn't handle non-finite values.
Results may differ from a plain program's by a relative error of at most 0.00023.
Values sent between devices are 32-bit elements; how exact they have to be, the bound alone decides.
No kernel may reach another device: no remote copies, remote signals or barrier semaphores. Data moves between devices by JAX's collectives and lax.ppermute only.
A program may use at most 64 MiB of HBM per device.

v0:
```python
import jax
import jax.numpy as jnp
from jax import lax
from jax.sharding import PartitionSpec as P

COLORS = 8
SWEEPS = 4


PRIOR_WEIGHT = 1.0


def from_behind(value, axis, steps):
    count = lax.axis_size(axis)
    pairs = [(source, (source + steps) % count) for source in range(count)]
    return lax.ppermute(value, axis, pairs)


def body(magnitudes, weights, slots, block_fields, owner, colors, color_terms):
    band_count = color_terms.shape[0]
    tiles = lax.axis_size("sky")
    my_tile = lax.axis_index("sky")
    my_band = lax.axis_index("band")
    band_mags, band_wts, band_slots = (magnitudes, weights, slots)
    own_row = 0
    band_rows, obs_count, star_count = band_mags.shape
    block_count, list_len = block_fields.shape
    block_rows = star_count // block_count
    fields = owner.shape[0]
    slot_grid = band_slots.reshape(band_rows, obs_count, block_count, block_rows)
    entries = jnp.arange(list_len, dtype=jnp.int32)
    star_weight = jnp.sum(band_wts, axis=1)
    mixing = (
        jnp.eye(band_count, dtype=jnp.float32)
        + color_terms
        - jnp.diag(jnp.sum(color_terms, axis=1))
    )
    owner_order = jnp.argsort(owner, stable=True)
    owned = fields // tiles

    def slot_sums(values):
        grid = values.reshape(band_rows, obs_count, block_count, block_rows)
        hits = slot_grid[..., None] == entries
        return jnp.sum(jnp.where(hits, grid[..., None], 0.0), axis=(1, 3))

    def spread(list_vals):
        hits = slot_grid[..., None] == entries
        picked = jnp.sum(jnp.where(hits, list_vals[:, None, :, None, :], 0.0), axis=4)
        return picked.reshape(band_rows, obs_count, star_count)

    def predict(zp_obs):
        star_means = jnp.sum(band_wts * (band_mags - zp_obs), axis=1) / star_weight
        all_means = lax.all_gather(star_means, "band", axis=0, tiled=True)
        mix_row = lax.dynamic_index_in_dim(mixing, my_band, 0, keepdims=True)
        predicted = jnp.dot(mix_row, all_means, precision=lax.Precision.HIGHEST)
        return (star_means, predicted)

    positions = jnp.argsort(owner_order, stable=True)
    rank_in = positions - owner * owned
    live = block_fields < fields
    safe_ids = jnp.minimum(block_fields, fields - 1)
    relative = jnp.mod(jnp.take(owner, safe_ids) - my_tile + 1, tiles)
    list_ids = jnp.where(live, relative * owned + jnp.take(rank_in, safe_ids), 3 * owned)
    segments = 3 * owned
    nearby_idx = jnp.mod(my_tile + jnp.arange(3, dtype=jnp.int32) - 1, tiles)
    near_fields = jnp.take(owner_order.reshape(tiles, owned), nearby_idx, axis=0)
    zp_colors = jnp.take(colors, near_fields)[None]
    zero_pts = jnp.zeros((band_rows, 3, owned), jnp.float32)

    def flatten(table):
        return table.reshape(band_rows, 3 * owned)

    def combine(partial_flat):
        partial_sums = partial_flat.reshape(band_rows, 3, owned)
        from_left = from_behind(partial_sums[:, 1:3], "sky", 1)
        from_right = from_behind(partial_sums[:, 0:2], "sky", -1)
        far_left = from_behind(partial_sums[:, 2], "sky", 2)
        far_right = from_behind(partial_sums[:, 0], "sky", -2)
        below = far_left + from_left[:, 0] + partial_sums[:, 0]
        middle = from_left[:, 1] + partial_sums[:, 1] + from_right[:, 0]
        above = partial_sums[:, 2] + from_right[:, 1] + far_right
        return jnp.stack([below, middle, above], axis=1)

    def lookup(table):
        padded = jnp.concatenate([flatten(table), jnp.zeros((band_rows, 1), jnp.float32)], axis=1)
        return spread(jnp.take(padded, list_ids, axis=1))

    def segment_band(per_band):
        return jax.ops.segment_sum(
            per_band.reshape(-1), list_ids.reshape(-1), num_segments=segments + 1
        )[:segments]

    def totals(values):
        per_slot = slot_sums(values)
        return combine(jax.vmap(segment_band)(per_slot))

    denominators = totals(band_wts) + PRIOR_WEIGHT

    def squared_misfit(residual, zp_obs):
        per_band = jnp.sum(band_wts * (residual - zp_obs) ** 2, axis=(1, 2))
        return lax.dynamic_index_in_dim(per_band, own_row, 0, keepdims=False)

    def advance(table, color_no):
        zp_obs = lookup(table)
        star_means, predicted = predict(zp_obs)
        residual = band_mags - predicted[:, None, :]
        updated = totals(band_wts * residual) / denominators
        local_value = squared_misfit(residual, zp_obs)
        return (jnp.where(zp_colors == color_no, updated, table), local_value)

    def later_colors(color_no, table):
        return advance(table, color_no)[0]

    def record(local_value):
        return lax.psum(local_value, "sky")

    recorded = []
    for sweep_no in range(SWEEPS):
        zero_pts, local_value = advance(zero_pts, 0)
        if sweep_no > 0:
            recorded.append(record(local_value))
        zero_pts = lax.fori_loop(1, COLORS, later_colors, zero_pts)
    zp_obs = lookup(zero_pts)
    star_means, predicted = predict(zp_obs)
    residual = band_mags - predicted[:, None, :]
    recorded.append(record(squared_misfit(residual, zp_obs)))
    stacked = jnp.stack(recorded)
    misfit = stacked / (obs_count * star_count * tiles)
    own_zp = lax.dynamic_index_in_dim(zero_pts[:, 1], own_row, 0, keepdims=True)
    own_means = lax.dynamic_index_in_dim(star_means, own_row, 0, keepdims=True)
    return (own_zp, own_means, misfit[:, None])


def solution(mesh):
    in_specs = (
        P("band", None, "sky"),
        P("band", None, "sky"),
        P("band", None, "sky"),
        P("sky", None),
        P(),
        P(),
        P(),
    )
    out_specs = (P("band", "sky"), P("band", "sky"), P(None, "band"))
    return jax.shard_map(body, mesh=mesh, in_specs=in_specs, out_specs=out_specs, check_vma=False)
```

profile of v0, /device:TPU:0, one launch (start us, length us, event | category | flops | bytes accessed | tf_op | source)
XLA Modules:
  0.0 838.4 jit_solution(8149706508148525772)
XLA Ops:
  0.7 6.5 sort.31
  7.2 5.8 sort.32
  20.3 6.2 all-gather.4
  42.8 8.4 gather_fusion.5
  60.7 166.6 %while.68 = (s32[]{:T(128)}, f32[1,3,512]{2,1,0:T(4,128)S(1)}, s32[1,3,512]{2,1,0:T(4,128)S(1)}, s32[8,32]{1,0:T(8,128)S(1)}, s32[1,8,2048]{2,1,0:T(8,128)S(1)},...) while((s32[]{:T(128)}, f32[1,3,512]{2,1,0:T(4,128)S(1)}, ...), condition=%wide.wide.region_15.18_spmd.clone, body=%wide.wide.region_10.17_spmd.clone.sunk | while | flops 3325443 | bytes 1340753 | solution.py:122
  63.3 5.2 all-gather.21
  86.6 5.2 all-gather.21
  111.2 5.2 all-gather.21
  134.4 5.2 all-gather.21
  159.0 5.2 all-gather.21
  182.2 5.2 all-gather.21
  206.7 5.2 all-gather.21
  229.8 5.2 all-gather.5
  249.6 170.6 %while.69 = (s32[]{:T(128)}, f32[1,3,512]{2,1,0:T(4,128)S(1)}, s32[1,3,512]{2,1,0:T(4,128)S(1)}, s32[8,32]{1,0:T(8,128)S(1)}, s32[1,8,2048]{2,1,0:T(8,128)S(1)},...) while((s32[]{:T(128)}, f32[1,3,512]{2,1,0:T(4,128)S(1)}, ...), condition=%wide.wide.region_25.28_spmd.clone, body=%wide.wide.region_20.27_spmd.clone.sunk | while | flops 3325443 | bytes 1471825 | solution.py:122
  252.3 5.2 all-gather.22
  279.6 5.2 all-gather.22
  302.7 5.2 all-gather.22
  327.4 5.2 all-gather.22
  350.5 5.2 all-gather.22
  375.2 5.2 all-gather.22
  398.3 5.2 all-gather.22
  422.8 5.4 all-gather.6
  442.9 170.6 %while.70 = (s32[]{:T(128)}, f32[1,3,512]{2,1,0:T(4,128)S(1)}, s32[1,3,512]{2,1,0:T(4,128)S(1)}, s32[8,32]{1,0:T(8,128)S(1)}, s32[1,8,2048]{2,1,0:T(8,128)S(1)},...) while((s32[]{:T(128)}, f32[1,3,512]{2,1,0:T(4,128)S(1)}, ...), condition=%wide.wide.region_35.38_spmd.clone, body=%wide.wide.region_30.37_spmd.clone.sunk | while | flops 3325443 | bytes 1471825 | solution.py:122
  445.5 5.2 all-gather.23
  472.9 5.2 all-gather.23
  496.0 5.2 all-gather.23
  520.6 5.2 all-gather.23
  543.7 5.2 all-gather.23
  568.4 5.2 all-gather.23
  591.5 5.2 all-gather.23
  635.9 170.9 %while.71 = (s32[]{:T(128)}, f32[1,3,512]{2,1,0:T(4,128)S(1)}, s32[1,3,512]{2,1,0:T(4,128)S(1)}, s32[8,32]{1,0:T(8,128)S(1)}, s32[1,8,2048]{2,1,0:T(8,128)S(1)},...) while((s32[]{:T(128)}, f32[1,3,512]{2,1,0:T(4,128)S(1)}, ...), condition=%wide.wide.region_45.48_spmd.clone, body=%wide.wide.region_40.47_spmd.clone.sunk | while | flops 3325443 | bytes 1471825 | solution.py:122
  816.5 18.4 %all-reduce = (f32[1,1]{0,1:T(1,128)}, f32[1,1]{0,1:T(1,128)}, f32[1,1]{0,1:T(1,128)}, f32[1,1]{0,1:T(1,128)}) all-reduce(f32[1,1]{0,1:T(1,128)} %bitcast.70, f32[1,1]{0,1:T(1,128)} %bitcast.66, f32[1,1]{0,1:T(1,128)} %bitcast.65, f32[1,1]{0,1:T(1,128)} %bitcast.64), channel_id=1, replica_groups=mesh['sky'=8,'band'=4] {'sky'}, use_global_device_ids=true, to_apply=%region_55.58 | all-reduce | flops 4 | bytes 32 | tf_op jit(solution)/shard_map/psum | solution.py:115
  (1206 shorter events, 667.2 us)
Async XLA Ops:
  29.9 21.3 %collective-permute-start.21 = (f32[1,2,512]{2,1,0:T(2,128)S(1)}, f32[1,2,512]{2,1,0:T(2,128)S(1)}, u32[]{:S(2)}, u32[]{:S(2)}) collective-permute-start(f32[1,2,512]{2,1,0:T(2,128)S(1)} %get-tuple-element.1354), channel_id=1, source_target_pairs={{0,4},{4,8},{8,12},{12,16},{16,20},{20,24},{24,28},{28,0},{1,5},{5... | collective-permute-start | bytes 12296 | tf_op jit(solution)/shard_map/ppermute | solution.py:16
  31.9 19.3 %collective-permute-start.22 = (f32[1,2,512]{2,1,0:T(2,128)S(1)}, f32[1,2,512]{2,1,0:T(2,128)S(1)}, u32[]{:S(2)}, u32[]{:S(2)}) collective-permute-start(f32[1,2,512]{2,1,0:T(2,128)S(1)} %get-tuple-element.1355), channel_id=1, source_target_pairs={{0,28},{4,0},{8,4},{12,8},{16,12},{20,16},{24,20},{28,24},{1,29},{... | collective-permute-start | bytes 12296 | tf_op jit(solution)/shard_map/ppermute | solution.py:16
  37.2 17.9 %collective-permute-start.17 = (f32[1,2,512]{2,1,0:T(2,128)S(1)}, f32[1,2,512]{2,1,0:T(2,128)S(1)}, u32[]{:S(2)}, u32[]{:S(2)}) collective-permute-start(f32[1,2,512]{2,1,0:T(2,128)S(1)} %get-tuple-element.1361), channel_id=1, source_target_pairs={{0,4},{4,8},{8,12},{12,16},{16,20},{20,24},{24,28},{28,0},{1,5},{5... | collective-permute-start | bytes 12296 | tf_op jit(solution)/shard_map/ppermute | solution.py:16
  37.3 17.8 %collective-permute-start.18 = (f32[1,2,512]{2,1,0:T(2,128)S(1)}, f32[1,2,512]{2,1,0:T(2,128)S(1)}, u32[]{:S(2)}, u32[]{:S(2)}) collective-permute-start(f32[1,2,512]{2,1,0:T(2,128)S(1)} %get-tuple-element.1362), channel_id=1, source_target_pairs={{0,28},{4,0},{8,4},{12,8},{16,12},{20,16},{24,20},{28,24},{1,29},{... | collective-permute-start | bytes 12296 | tf_op jit(solution)/shard_map/ppermute | solution.py:16
  51.2 7.9 collective-permute-start.20
  51.3 7.9 collective-permute-start.23
  72.2 6.3 collective-permute-start.1
  96.8 6.3 collective-permute-start.1
  120.0 6.3 collective-permute-start.1
  144.5 6.3 collective-permute-start.1
  167.7 6.3 collective-permute-start.1
  192.3 6.3 collective-permute-start.1
  215.5 6.3 collective-permute-start.1
  237.8 6.4 collective-permute-start.25
  265.2 6.3 collective-permute-start.5
  288.3 6.3 collective-permute-start.5
  312.9 6.3 collective-permute-start.5
  336.1 6.3 collective-permute-start.5
  360.7 6.3 collective-permute-start.5
  383.8 6.3 collective-permute-start.5
  408.5 6.3 collective-permute-start.5
  431.0 6.4 collective-permute-start.29
  481.5 6.3 collective-permute-start.9
  529.3 6.3 collective-permute-start.9
  601.7 6.3 collective-permute-start.9
  624.0 6.4 collective-permute-start.33
  646.6 6.4 collective-permute-start.12
  674.8 6.3 collective-permute-start.13
  699.4 6.3 collective-permute-start.13
  722.5 6.3 collective-permute-start.13
  747.2 6.3 collective-permute-start.13
  794.9 6.3 collective-permute-start.13
  (108 other events, 589.1 us)
where the time goes:
time: 846 us; the launch traced here: 838 us
  starting transfers between devices  220 us (26%)
  waiting for transfers between devices  212 us (25%)
  blocking collectives  191 us (23%)
  other arithmetic  120 us (14%)
  local copies, waits for them, and re-layouts  82.9 us (10%)
    ppermute x132, starting transfers between devices, from_behind(): return lax.ppermute(value, axis, pairs)  220 us
    ppermute x132, waiting for transfers between devices, from_behind(): return lax.ppermute(value, axis, pairs)  212 us
    all_gather x33, blocking collectives, predict(): all_means = lax.all_gather(star_means, 'band', axis=0, tiled=True)  172 us
    scatter-add x33, other arithmetic, segment_band(): jax.ops.segment_sum(per_band.reshape(-1), list_ids.reshape(-1), num_segme...  67.3 us
    gather x66, local copies, waits for them, and re-layouts, lookup(): return spread(jnp.take(padded, list_ids, axis=1))  59.3 us
    psum x1, blocking collectives, record(): return lax.psum(local_value, 'sky')  18.4 us
    reduce_sum x33, other arithmetic, spread(): jnp.sum(jnp.where(hits, list_vals[:, None, :, None, :], 0.0), axis=4)  18.2 us
  transfers between devices with their start and end apart: 132, of which 91 were waited for; matrix products, arithmetic and copies ran while one was open for 1% of the time, Pallas kernels for 0%

commit v1 on v0

--- a/solution.py
+++ b/solution.py
@@ -1,6 +1,10 @@
+import functools
+
 import jax
 import jax.numpy as jnp
 from jax import lax
+from jax.experimental import pallas as pl
+from jax.experimental.pallas import tpu as pltpu
 from jax.sharding import PartitionSpec as P
 
 COLORS = 8
@@ -8,6 +12,478 @@
 
 
 PRIOR_WEIGHT = 1.0
+LANES = 128
+SUBS = 8
+HALF = LANES // 2
+FOLD = 3
+F32 = jnp.float32
+BF16 = jnp.bfloat16
+I32 = jnp.int32
+NT = (((1,), (1,)), ((), ()))
+NN = (((1,), (0,)), ((), ()))
+
+
+def iota(shape, axis):
+    return lax.broadcasted_iota(I32, shape, axis)
+
+
+def pick(table, idx):
+    return jnp.take_along_axis(table, idx, axis=1, mode="promise_in_bounds")
+
+
+def row_to(value, rows):
+    return jnp.broadcast_to(value, (rows, value.shape[1]))
+
+
+def table_lookup(table_ref, ids, rows, init):
+    out = jnp.full(ids.shape, init, F32)
+    for r in range(rows):
+        hit = pick(row_to(table_ref[r : r + 1, :], ids.shape[0]), ids & (LANES - 1))
+        out = jnp.where((ids >> 7) == r, hit, out)
+    return out
+
+
+def tile_kernel(
+    dims, mix_ref, band_ref, raw_ref, mag_ref, lists_ref, colors_ref, out_ref, tab_ref, pad_ref, sq_ref, wf_ref, x_ref, colf_ref
+):
+    bands, obs, stars, blocks, entries, fields, blk_rows = dims
+    lane = iota((SUBS, LANES), 1)
+    pad_ref[...] = jnp.full((SUBS, LANES), fields, I32)
+    pad_ref[:, :entries] = lists_ref[...]
+    ids = pad_ref[...]
+    live = ids < fields
+    safe = jnp.where(live, ids, 0)
+    colf_ref[...] = colors_ref[...].astype(F32)
+    color = table_lookup(colf_ref, safe, fields // LANES, 0.0).astype(I32)
+    key = jnp.where(live, color * entries + lane, COLORS * entries)
+    rank = jnp.zeros((SUBS, LANES), I32)
+    for e in range(entries):
+        rank = rank + jnp.where(key[:, e : e + 1] < key, 1, 0)
+    live_f = jnp.where(live, 1.0, 0.0)
+    dead = entries - jnp.sum(live_f, axis=1, keepdims=True).astype(I32)
+    pos = jnp.where(live, rank + ((dead * color) >> (COLORS.bit_length() - 1)), 4 * LANES)
+    inv = jnp.full((SUBS, LANES), -1, I32)
+    for e in range(entries):
+        inv = jnp.where(pos[:, e : e + 1] == lane, e, inv)
+    used = inv >= 0
+    inv_safe = jnp.where(used, inv, 0)
+    fpos = jnp.where(used, pick(ids, inv_safe).astype(F32), -1.0)
+    cpos = jnp.where(used, pick(color, inv_safe).astype(F32), float(COLORS))
+    pos_live = jnp.where(live, pos, 0)
+    tab_ref[...] = ((pos_live >> 1) & 1) * HALF + (pos_live >> 2) * (2 * bands) + (pos_live & 1) * bands
+
+    sq_ref[...] = jnp.zeros((LANES, LANES), F32)
+    sq_ref[0:SUBS, :] = inv.astype(F32)
+    inv_t = sq_ref[...].T
+    mine = band_ref[0]
+    lanes_sq = iota((entries, LANES), 1)
+    t0_cols = jnp.zeros((entries, LANES), F32)
+    wt_cols = jnp.zeros((entries, LANES), F32)
+    for blk in range(blocks):
+        lo, hi = blk * blk_rows, (blk + 1) * blk_rows
+        inv_col = jnp.broadcast_to(inv_t[0:entries, blk : blk + 1], (entries, blk_rows))
+        pred = jnp.zeros((1, blk_rows), F32)
+        for b in range(bands):
+            w = raw_ref[b, 0:obs, lo:hi]
+            slot = raw_ref[b, obs : 2 * obs, lo:hi]
+            acc = jnp.zeros((entries, blk_rows), F32)
+            for k in range(obs):
+                acc = acc + jnp.where(slot[k : k + 1] == inv_col, w[k : k + 1], 0.0)
+            scale = mix_ref[b] / jnp.sum(w, axis=0, keepdims=True)
+            wf_ref[b * entries : (b + 1) * entries, :] = acc
+            x_ref[b * entries : (b + 1) * entries, :] = acc * scale
+            pieces = blk_rows // LANES
+            means = raw_ref[b, blk * pieces : (blk + 1) * pieces, stars : stars + LANES]
+            pred = pred + mix_ref[b] * jnp.concatenate([means[i : i + 1] for i in range(pieces)], axis=1)
+        own = wf_ref[pl.ds(mine * entries, entries), :]
+        gram = lax.dot_general(own, x_ref[...], NT, precision=lax.Precision.HIGHEST, preferred_element_type=F32)
+        out_ref[pl.ds(blk, entries, stride=SUBS), :] = gram
+        w = raw_ref[mine, 0:obs, lo:hi]
+        slot = raw_ref[mine, obs : 2 * obs, lo:hi]
+        value = w * (mag_ref[:, lo:hi] - pred)
+        acc = jnp.zeros((entries, blk_rows), F32)
+        for k in range(obs):
+            acc = acc + jnp.where(slot[k : k + 1] == inv_col, value[k : k + 1], 0.0)
+        t0_cols = jnp.where(lanes_sq == blk, jnp.sum(acc, axis=1, keepdims=True), t0_cols)
+        wt_cols = jnp.where(lanes_sq == blk, jnp.sum(own, axis=1, keepdims=True), wt_cols)
+    sq_ref[...] = jnp.zeros((LANES, LANES), F32)
+    sq_ref[0:entries, :] = t0_cols
+    sq_ref[entries : 2 * entries, :] = wt_cols
+    flipped = sq_ref[...].T[0:SUBS]
+    extra = jnp.where(lane < 3 * entries, pltpu.roll(fpos, 2 * entries, 1), pltpu.roll(cpos, 3 * entries, 1))
+    out_ref[entries * SUBS : (entries + 1) * SUBS, :] = jnp.where(lane < 2 * entries, flipped, extra)
+
+
+def split3(value):
+    hi = value.astype(BF16).astype(F32)
+    rest = value - hi
+    mid = rest.astype(BF16).astype(F32)
+    return hi, mid, rest - mid
+
+
+def sweep_kernel(
+    dims, mix_ref, place_ref, all_ref, raw_ref, mag_ref, tab_ref, owner_ref,
+    zp_ref, means_ref, misfit_ref,
+    et_ref, v_ref, den_ref, fld_ref, col_ref, g_ref, s_ref, z_ref, dz_ref, zs_ref,
+    sq_ref, lim_ref, fc_ref, fr_ref, tv_ref, ze_ref, rk_ref, big_ref,
+):
+    tiles, bands, obs, stars, blocks, entries, fields, blk_rows, owned = dims
+    groups = entries // 4
+    pair = 2 * bands
+    vrows = groups * pair
+    rows_dev = (entries + 1) * SUBS
+    lane8 = iota((SUBS, LANES), 1)
+    low8 = lane8 < HALF
+    my_tile, mine = place_ref[0], place_ref[1]
+
+    for b in range(bands):
+        sq_ref[...] = jnp.zeros((LANES, LANES), F32)
+        for t in range(tiles):
+            sq_ref[t * SUBS : (t + 1) * SUBS, :] = all_ref[t * bands + b, entries * SUBS : rows_dev, :]
+        et_ref[...] = sq_ref[...].T
+        for p in range(2):
+            for q, dest in enumerate((v_ref, den_ref, fld_ref, col_ref)):
+                first = et_ref[pl.ds(q * entries + p, groups, stride=4), :]
+                second = et_ref[pl.ds(q * entries + 2 + p, groups, stride=4), :]
+                dest[pl.ds(p * bands + b, groups, stride=pair), :] = jnp.where(low8, first, pltpu.roll(second, HALF, 1))
+
+    def turn(k, carry):
+        for p in range(2):
+            for b in range(bands):
+                parts = []
+                for half in range(2):
+                    start = pl.multiple_of((4 * k + 2 * half + p) * SUBS, SUBS)
+                    for t in range(tiles):
+                        parts.append(all_ref[t * bands + b, pl.ds(start, SUBS), :])
+                flipped = jnp.concatenate(parts, axis=0).T
+                for b2 in range(bands):
+                    g_ref[pl.ds(b2 * vrows + k * pair + p * bands + b, entries, stride=bands * vrows), :] = flipped[
+                        b2 * entries : (b2 + 1) * entries
+                    ]
+        return carry
+
+    lax.fori_loop(0, groups, turn, 0)
+
+    srows = 2 * groups
+    fld2 = fld_ref[pl.ds(0, srows, stride=bands), :]
+    col2 = col_ref[pl.ds(0, srows, stride=bands), :]
+    row2 = iota((srows, LANES), 0)
+    position = 4 * (row2 >> 1) + 2 * jnp.where(iota((srows, LANES), 1) < HALF, 0, 1) + (row2 & 1)
+    most = jnp.zeros((1, LANES), F32)
+    for c in range(COLORS):
+        hit = col2 == float(c)
+        lim_ref[0, c] = jnp.min(jnp.where(hit, position, entries))
+        lim_ref[1, c] = jnp.max(jnp.where(hit, position + 1, 0))
+        count = jnp.sum(jnp.where(hit, 1.0, 0.0), axis=0, keepdims=True)
+        most = jnp.maximum(most, count + pltpu.roll(count, HALF, 1))
+    fits = jnp.max(most) <= 4.0 * FOLD
+
+    def build(c, carry):
+        hit = col2 == c.astype(F32)
+        chosen = jnp.where(hit, fld2, -1.0)
+        folded = []
+        for m in range(FOLD):
+            for p in range(2):
+                best = jnp.full((1, LANES), -1.0, F32)
+                for k in range(m, groups, FOLD):
+                    best = jnp.maximum(best, chosen[2 * k + p : 2 * k + p + 1])
+                folded.append(best)
+        sq_ref[0 : 2 * FOLD, :] = jnp.concatenate(folded, axis=0)
+        columns = sq_ref[...].T
+        for i in range(2 * FOLD):
+            col = jnp.broadcast_to(columns[:, i : i + 1], (LANES, LANES))
+            for j in range(2 * FOLD):
+                row = jnp.where(folded[j] < 0.0, -2.0, folded[j])
+                tile = jnp.where(col == row, 1.0, 0.0).astype(BF16)
+                m, p, n, r = i // 2, i % 2, j // 2, j % 2
+                s_ref[c * FOLD * FOLD + m * FOLD + n, p * LANES : (p + 1) * LANES, r * LANES : (r + 1) * LANES] = tile
+        return carry
+
+    lax.fori_loop(0, COLORS, build, 0)
+
+    def spread_rows(value):
+        flat = jnp.concatenate([value[0:bands], value[bands:pair]], axis=1)
+        hi, mid, lo = split3(flat)
+        return jnp.concatenate([hi, mid, lo, jnp.zeros_like(hi)], axis=0).astype(BF16)
+
+    def pack_rows(total):
+        flat = total[0:bands] + (total[bands : 2 * bands] + total[2 * bands : 3 * bands])
+        return jnp.concatenate([flat[:, :LANES], flat[:, LANES:]], axis=0)
+
+    def same_field(c, src):
+        cf = c.astype(F32)
+
+        @pl.when(fits)
+        def fast():
+            lhs = []
+            for m in range(FOLD):
+                fold = jnp.zeros((pair, LANES), F32)
+                for k in range(m, groups, FOLD):
+                    rows = slice(k * pair, (k + 1) * pair)
+                    fold = fold + jnp.where(col_ref[rows] == cf, src[rows], 0.0)
+                lhs.append(spread_rows(fold))
+            for n in range(FOLD):
+                total = jnp.zeros((4 * bands, 2 * LANES), F32)
+                for m in range(FOLD):
+                    total = total + lax.dot_general(
+                        lhs[m], s_ref[c * FOLD * FOLD + m * FOLD + n], NN, preferred_element_type=F32
+                    )
+                packed = pack_rows(total)
+                for k in range(n, groups, FOLD):
+                    tv_ref[k * pair : (k + 1) * pair, :] = packed
+
+        @pl.when(jnp.logical_not(fits))
+        def general():
+            chosen = jnp.where(col2 == cf, fld2, -1.0)
+            sq_ref[...] = jnp.full((LANES, LANES), -1.0, F32)
+            sq_ref[0:srows, :] = chosen
+            columns = sq_ref[...].T
+            for i in range(srows):
+                fc_ref[i] = jnp.broadcast_to(columns[:, i : i + 1], (LANES, LANES))
+                fr_ref[i] = row_to(jnp.where(chosen[i : i + 1] < 0.0, -2.0, chosen[i : i + 1]), SUBS)
+            for m in range(groups):
+                rows = slice(m * pair, (m + 1) * pair)
+                big_ref[m] = spread_rows(jnp.where(col_ref[rows] == cf, src[rows], 0.0)).astype(F32)
+
+            def outer(n, carry):
+                def inner(m, total):
+                    parts = []
+                    for r in range(2):
+                        row = fr_ref[2 * n + r][0:1]
+                        upper = jnp.where(fc_ref[2 * m] == row, 1.0, 0.0)
+                        lower = jnp.where(fc_ref[2 * m + 1] == row, 1.0, 0.0)
+                        lhs = big_ref[m].astype(BF16)
+                        parts.append(
+                            lax.dot_general(lhs[:, :LANES], upper.astype(BF16), NN, preferred_element_type=F32)
+                            + lax.dot_general(lhs[:, LANES:], lower.astype(BF16), NN, preferred_element_type=F32)
+                        )
+                    return total + jnp.concatenate(parts, axis=1)
+
+                total = lax.fori_loop(0, groups, inner, jnp.zeros((4 * bands, 2 * LANES), F32))
+                tv_ref[pl.ds(pl.multiple_of(n * pair, pair), pair), :] = pack_rows(total)
+                return carry
+
+            lax.fori_loop(0, groups, outer, 0)
+
+    z_ref[...] = jnp.full((vrows, LANES), PRIOR_WEIGHT, F32)
+
+    def denominator(c, carry):
+        same_field(c, den_ref)
+        z_ref[...] = z_ref[...] + jnp.where(col_ref[...] == c.astype(F32), tv_ref[...], 0.0)
+        return carry
+
+    lax.fori_loop(0, COLORS, denominator, 0)
+    den_ref[...] = 1.0 / z_ref[...]
+    z_ref[...] = jnp.zeros((vrows, LANES), F32)
+
+    def step(n, carry):
+        c = n & (COLORS - 1)
+        cf = c.astype(F32)
+        same_field(c, v_ref)
+        for k in range(groups):
+            rows = slice(k * pair, (k + 1) * pair)
+            old = z_ref[rows]
+            new = jnp.where(col_ref[rows] == cf, tv_ref[rows] * den_ref[rows], old)
+            z_ref[rows] = new
+            diff = new - old
+            turned = pltpu.roll(diff, HALF, 1)
+            dz_ref[2 * k * pair : (2 * k + 1) * pair, :] = jnp.where(low8, diff, turned)
+            dz_ref[(2 * k + 1) * pair : (2 * k + 2) * pair, :] = jnp.where(low8, turned, diff)
+
+        def apply(p, accs):
+            accs = list(accs)
+            for b2 in range(bands):
+                j = p * bands + b2
+                row = row_to(dz_ref[pl.ds(j, 1), :], pair)
+                for k in range(groups):
+                    base = pl.multiple_of(j * vrows + k * pair, pair)
+                    accs[k] = accs[k] + g_ref[pl.ds(base, pair), :] * row
+            return tuple(accs)
+
+        start = tuple(v_ref[k * pair : (k + 1) * pair] for k in range(groups))
+        done = lax.fori_loop(lim_ref[0, c], lim_ref[1, c], apply, start)
+        for k in range(groups):
+            v_ref[k * pair : (k + 1) * pair, :] = done[k]
+
+        @pl.when(c == COLORS - 1)
+        def keep():
+            zs_ref[n >> (COLORS.bit_length() - 1)] = z_ref[...]
+
+        return carry
+
+    lax.fori_loop(0, SWEEPS * COLORS, step, 0)
+
+    tab = tab_ref[...]
+    for sweep in range(SWEEPS):
+        sq_ref[...] = jnp.zeros((LANES, LANES), F32)
+        sq_ref[0:vrows, :] = zs_ref[sweep]
+        et_ref[...] = sq_ref[...].T
+        first = et_ref[pl.ds(pl.multiple_of(my_tile * SUBS, SUBS), SUBS), :]
+        second = et_ref[pl.ds(pl.multiple_of(HALF + my_tile * SUBS, SUBS), SUBS), :]
+        table = jnp.where(low8, first, pltpu.roll(second, HALF, 1))
+        for b in range(bands):
+            ze_ref[sweep * bands + b] = pick(table, tab + b)
+
+    squares = [jnp.zeros((obs, LANES), F32) for _ in range(SWEEPS)]
+    for chunk in range(stars // LANES):
+        at = slice(chunk * LANES, (chunk + 1) * LANES)
+        blk = chunk * LANES // blk_rows
+        pred = [jnp.zeros((1, LANES), F32) for _ in range(SWEEPS)]
+        own_mean = jnp.zeros((1, LANES), F32)
+        for b in range(bands):
+            w = raw_ref[b, 0:obs, at]
+            slot = raw_ref[b, obs : 2 * obs, at].astype(I32)
+            inverse = 1.0 / jnp.sum(w, axis=0, keepdims=True)
+            base = raw_ref[b, chunk : chunk + 1, stars : stars + LANES]
+            for sweep in range(SWEEPS):
+                seen = pick(row_to(ze_ref[sweep * bands + b, blk : blk + 1, :], obs), slot)
+                mean = base - jnp.sum(w * seen, axis=0, keepdims=True) * inverse
+                pred[sweep] = pred[sweep] + mix_ref[b] * mean
+                if sweep == SWEEPS - 1:
+                    own_mean = jnp.where(mine == b, mean, own_mean)
+        means_ref[0:1, at] = own_mean
+        w = raw_ref[mine, 0:obs, at]
+        slot = raw_ref[mine, obs : 2 * obs, at].astype(I32)
+        mag = mag_ref[:, at]
+        for sweep in range(SWEEPS):
+            seen = pick(row_to(ze_ref[sweep * bands + mine, blk : blk + 1, :], obs), slot)
+            gap = mag - pred[sweep] - seen
+            squares[sweep] = squares[sweep] + w * gap * gap
+    result = jnp.zeros((SUBS, LANES), F32)
+    for sweep in range(SWEEPS):
+        result = jnp.where(lane8 == sweep, jnp.sum(squares[sweep]), result)
+    misfit_ref[...] = result
+
+    frows = fields // LANES
+    own = jnp.where(owner_ref[...] == my_tile, 1.0, 0.0)
+    upto = jnp.where(iota((LANES, LANES), 0) <= iota((LANES, LANES), 1), 1.0, 0.0).astype(BF16)
+    inside = lax.dot_general(own.astype(BF16), upto, NN, preferred_element_type=F32)
+    sums = jnp.broadcast_to(jnp.sum(own, axis=1, keepdims=True), (frows, LANES))
+    before = jnp.where(iota((frows, frows), 1) < iota((frows, frows), 0), 1.0, 0.0).astype(BF16)
+    ahead = lax.dot_general(before, sums.astype(BF16), NN, preferred_element_type=F32)
+    rk_ref[...] = jnp.where(own > 0.0, inside + ahead - 1.0, -1.0)
+    ids = jnp.where(fld2 < 0.0, 0.0, fld2).astype(I32)
+    ranks = jnp.where(fld2 < 0.0, -1.0, table_lookup(rk_ref, ids, frows, -1.0))
+    sq_ref[...] = jnp.full((LANES, LANES), -1.0, F32)
+    sq_ref[0:srows, :] = ranks
+    columns = sq_ref[...].T
+    hi, mid, lo = split3(z_ref[pl.ds(mine, srows, stride=bands), :])
+    places = iota((LANES, owned), 1).astype(F32)
+    ones = jnp.ones((1, LANES), F32)
+    total = jnp.zeros((SUBS, owned), F32)
+    for r in range(srows):
+        one_hot = jnp.where(jnp.broadcast_to(columns[:, r : r + 1], (LANES, owned)) == places, 1.0, 0.0)
+        lhs = jnp.concatenate([hi[r : r + 1], mid[r : r + 1], lo[r : r + 1], ones, jnp.zeros((4, LANES), F32)], axis=0)
+        total = total + lax.dot_general(lhs.astype(BF16), one_hot.astype(BF16), NN, preferred_element_type=F32)
+    zp_ref[...] = (total[0:1] + (total[1:2] + total[2:3])) / jnp.maximum(total[3:4], 1.0)
+
+
+def vmem():
+    return pl.BlockSpec(memory_space=pltpu.VMEM)
+
+
+def smem():
+    return pl.BlockSpec(memory_space=pltpu.SMEM)
+
+
+def replicate(payload):
+    return lax.all_gather(payload, ("sky", "band"), axis=0)
+
+
+def sky_sum(value):
+    return lax.psum(value, "sky")
+
+
+def local_body(magnitudes, weights, slots, block_fields, owner, colors, color_terms):
+    bands = color_terms.shape[0]
+    tiles = lax.axis_size("sky")
+    my_tile = lax.axis_index("sky")
+    my_band = lax.axis_index("band")
+    _, obs, stars = magnitudes.shape
+    blocks, entries = block_fields.shape
+    fields = owner.shape[0]
+    blk_rows = stars // blocks
+    owned = fields // tiles
+    mags, wts, slt = magnitudes[0], weights[0], slots[0]
+    base = jnp.sum(wts * mags, axis=0) / jnp.sum(wts, axis=0)
+    mixing = jnp.eye(bands, dtype=F32) + color_terms - jnp.diag(jnp.sum(color_terms, axis=1))
+    mix_row = lax.dynamic_index_in_dim(mixing, my_band, 0, keepdims=False)
+    left = jnp.concatenate([wts, slt.astype(F32)], axis=0)
+    raw = lax.all_gather(jnp.concatenate([left, base.reshape(2 * obs, LANES)], axis=1), "band", axis=0)
+    place = jnp.stack([my_tile, my_band]).astype(I32)
+
+    rows_dev = (entries + 1) * SUBS
+    payload, tab = pl.pallas_call(
+        functools.partial(tile_kernel, (bands, obs, stars, blocks, entries, fields, blk_rows)),
+        name="tile",
+        out_shape=(jax.ShapeDtypeStruct((rows_dev, LANES), F32), jax.ShapeDtypeStruct((SUBS, LANES), I32)),
+        in_specs=[smem(), smem(), vmem(), vmem(), vmem(), vmem()],
+        out_specs=(vmem(), vmem()),
+        scratch_shapes=[
+            pltpu.VMEM((SUBS, LANES), I32),
+            pltpu.VMEM((LANES, LANES), F32),
+            pltpu.VMEM((bands * entries, blk_rows), F32),
+            pltpu.VMEM((bands * entries, blk_rows), F32),
+            pltpu.VMEM((fields // LANES, LANES), F32),
+        ],
+    )(mix_row, place[1:], raw, mags, block_fields, colors.reshape(-1, LANES))
+
+    everything = replicate(payload)
+
+    groups = entries // 4
+    pair = 2 * bands
+    vrows = groups * pair
+    zp, means, partial = pl.pallas_call(
+        functools.partial(sweep_kernel, (tiles, bands, obs, stars, blocks, entries, fields, blk_rows, owned)),
+        name="sweeps",
+        out_shape=(
+            jax.ShapeDtypeStruct((1, owned), F32),
+            jax.ShapeDtypeStruct((1, stars), F32),
+            jax.ShapeDtypeStruct((SUBS, LANES), F32),
+        ),
+        in_specs=[smem(), smem()] + [vmem()] * 5,
+        out_specs=(vmem(), vmem(), vmem()),
+        scratch_shapes=[
+            pltpu.VMEM((LANES, LANES), F32),
+            pltpu.VMEM((vrows, LANES), F32),
+            pltpu.VMEM((vrows, LANES), F32),
+            pltpu.VMEM((vrows, LANES), F32),
+            pltpu.VMEM((vrows, LANES), F32),
+            pltpu.VMEM((bands * entries * vrows, LANES), F32),
+            pltpu.VMEM((COLORS * FOLD * FOLD, 2 * LANES, 2 * LANES), BF16),
+            pltpu.VMEM((vrows, LANES), F32),
+            pltpu.VMEM((bands * entries, LANES), F32),
+            pltpu.VMEM((SWEEPS, vrows, LANES), F32),
+            pltpu.VMEM((LANES, LANES), F32),
+            pltpu.SMEM((2, COLORS), I32),
+            pltpu.VMEM((2 * groups, LANES, LANES), F32),
+            pltpu.VMEM((2 * groups, SUBS, LANES), F32),
+            pltpu.VMEM((vrows, LANES), F32),
+            pltpu.VMEM((SWEEPS * bands, SUBS, LANES), F32),
+            pltpu.VMEM((fields // LANES, LANES), F32),
+            pltpu.VMEM((groups, 4 * bands, 2 * LANES), F32),
+        ],
+        compiler_params=pltpu.CompilerParams(vmem_limit_bytes=56 * 1024 * 1024),
+    )(mix_row, place, everything, raw, mags, tab, owner.reshape(-1, LANES))
+
+    misfit = sky_sum(partial[0, :SWEEPS]) / (obs * stars * tiles)
+    return zp, means, misfit[:, None]
+
+
+def fits_local(mesh, blocks_all, entries, stars, obs, bands, fields):
+    tiles = mesh.shape["sky"]
+    blocks = blocks_all // tiles
+    return (
+        2 * blocks_all == LANES
+        and blocks == SUBS
+        and bands * entries == LANES
+        and obs == SUBS
+        and 2 * bands == SUBS
+        and mesh.shape["band"] == bands
+        and stars // tiles == 2 * obs * LANES
+        and (stars // blocks_all) % LANES == 0
+        and fields % (tiles * LANES) == 0
+    )
 
 
 def from_behind(value, axis, steps):
@@ -16,7 +492,7 @@
     return lax.ppermute(value, axis, pairs)
 
 
-def body(magnitudes, weights, slots, block_fields, owner, colors, color_terms):
+def wide_body(magnitudes, weights, slots, block_fields, owner, colors, color_terms):
     band_count = color_terms.shape[0]
     tiles = lax.axis_size("sky")
     my_tile = lax.axis_index("sky")
@@ -142,4 +618,13 @@
         P(),
     )
     out_specs = (P("band", "sky"), P("band", "sky"), P(None, "band"))
-    return jax.shard_map(body, mesh=mesh, in_specs=in_specs, out_specs=out_specs, check_vma=False)
+
+    def call(magnitudes, weights, slots, block_fields, owner, colors, color_terms):
+        bands, obs, stars = magnitudes.shape
+        blocks_all, entries = block_fields.shape
+        local = fits_local(mesh, blocks_all, entries, stars, obs, bands, owner.shape[0])
+        body = local_body if local else wide_body
+        run = jax.shard_map(body, mesh=mesh, in_specs=in_specs, out_specs=out_specs, check_vma=False)
+        return run(magnitudes, weights, slots, block_fields, owner, colors, color_terms)
+
+    return call

time: 846 us -> 150 us (0.18)
  starting transfers between devices: 220 us -> 0.04 us
  blocking collectives: 191 us -> 29.2 us
  waiting for transfers between devices: 212 us -> 62.5 us
  other arithmetic: 120 us -> 6.08 us
  local copies, waits for them, and re-layouts: 82.9 us -> 1.27 us
  Pallas kernels: 0 us -> 36.3 us
  between operations: 1.92 us -> 14.1 us
    ppermute x132 -> x0, starting transfers between devices: 220 us -> none  [from_behind(): return lax.ppermute(value, axis, pairs)]
    ppermute x132 -> x0, waiting for transfers between devices: 212 us -> none  [from_behind(): return lax.ppermute(value, axis, pairs)]
    all_gather x33 -> x1, blocking collectives: 172 us -> 9.27 us  [local_body(): lax.all_gather(jnp.concatenate([left, base.reshape(2 * obs, LANES)], axis...]
    gather x73 -> x0, local copies, waits for them, and re-layouts: 71.9 us -> none  [the longest x66 59.3 us: lookup(): return spread(jnp.take(padded, list_ids, axis=1))]
    scatter-add x33 -> x0, other arithmetic: 67.3 us -> none  [segment_band(): jax.ops.segment_sum(per_band.reshape(-1), list_ids.reshape(-1), num_segme...]
    all_gather x0 -> x1, waiting for transfers between devices: none -> 62.5 us  [replicate(): return lax.all_gather(payload, ('sky', 'band'), axis=0)]
    pallas_call x0 -> x2, Pallas kernels: none -> 36.3 us  [the longest x1 31.7 us: local_body(): pl.pallas_call(functools.partial(sweep_kernel, (tiles, bands, obs, stars,...]
    reduce_sum x100 -> x3, other arithmetic: 33 us -> 2.56 us  [the longest x2 1.75 us: local_body(): base = jnp.sum(wts * mags, axis=0) / jnp.sum(wts, axis=0)]
  transfers between devices with their start and end apart: 132 -> 1, of which waited for: 91 -> 1; matrix products, arithmetic and copies ran while one was open for 1% -> 0% of each run, Pallas kernels for 0% -> 0%
where the time goes in v1:
time: 150 us; the launch traced here: 149 us
  waiting for transfers between devices  62.5 us (42%)
  Pallas kernels  36.3 us (24%)
  blocking collectives  29.2 us (19%)
  between operations  14.1 us (9%)
  other arithmetic  6.08 us (4%)
    all_gather x1, waiting for transfers between devices, replicate(): return lax.all_gather(payload, ('sky', 'band'), axis=0)  62.5 us
    pallas_call x1, Pallas kernels, local_body(): pl.pallas_call(functools.partial(sweep_kernel, (tiles, bands, obs, stars,...  31.7 us
    psum x1, blocking collectives, sky_sum(): return lax.psum(value, 'sky')  19.9 us
    all_gather x1, blocking collectives, local_body(): lax.all_gather(jnp.concatenate([left, base.reshape(2 * obs, LANES)], axis...  9.27 us
    pallas_call x1, Pallas kernels, local_body(): pl.pallas_call(functools.partial(tile_kernel, (bands, obs, stars, blocks,...  4.58 us
  transfers between devices with their start and end apart: 1, of which 1 were waited for; matrix products, arithmetic and copies ran while one was open for 0% of the time, Pallas kernels for 0%

profile of v1, /device:TPU:0, one launch (start us, length us, event | category | flops | bytes accessed | tf_op | source)
XLA Modules:
  0.0 149.4 jit_solution(14203431643701988990)
XLA Ops:
  7.2 0.0 all-gather.4.cloned.1.call-start
  7.2 0.8 reduce_sum.27
  8.0 0.8 select_subtract_fusion
  8.8 0.9 reduce_sum.29
  9.6 0.9 multiply_reduce_fusion
  10.5 0.8 convert_bitcast_fusion
  11.4 0.9 pad_maximum_fusion
  12.2 9.3 %all-gather = f32[64,2176]{1,0:T(8,128)} all-gather(f32[16,2176]{1,0:T(8,128)S(1)} %pad_maximum_fusion), channel_id=2, replica_groups=mesh['sky'=8,'band'=4] {'band'}, dimensions={0}, use_global_device_ids=true | all-gather | bytes 696320 | tf_op jit(solution)/shard_map/all_gather | solution.py:412
  21.5 0.6 dynamic-slice_bitcast_fusion.mix_ref
  22.1 4.6 %tile.1 = (f32[264,128]{1,0:T(8,128)}, s32[8,128]{1,0:T(8,128)}) custom-call(f32[4]{0:T(128)} %dynamic-slice_bitcast_fusion.mix_ref, s32[1]{0:T(128)} %bitcast.2.band_ref, f32[4,16,2176]{2,1,0:T(8,128)} %bitcast.20, f32[8,2048]{1,0:T(8,128)} %bitcast.23, s32[8,32]{1,0:T(8,128)} %lists_ref.1, s32[32,128]{1,0:T(8,128)} %bitcast.27), custom_call_target="tpu_custom_call" | custom-call | tf_op jit(solution)/shard_map/tile/pallas_call | solution.py:416
  26.7 0.0 all-gather.4.cloned.1.call-update
  26.7 0.6 pad_add_fusion.place_ref
  27.3 62.5 %all-gather.4.cloned.1.call-done = f32[8448,128]{1,0:T(8,128)} async-done(((f32[264,128]{1,0:T(8,128)}), f32[8448,128]{1,0:T(8,128)}) %all-gather.4.cloned.1.call-update) | async-done | bytes 4325392 | tf_op jit(solution)/shard_map/all_gather | solution.py:390
  89.8 31.7 %sweeps.1 = (f32[1,512]{1,0:T(1,128)}, f32[1,2048]{1,0:T(1,128)}, f32[8,128]{1,0:T(8,128)}) custom-call(f32[4]{0:T(128)} %dynamic-slice_bitcast_fusion.mix_ref, s32[2]{0:T(128)} %pad_add_fusion.place_ref, f32[32,264,128]{2,1,0:T(8,128)} %bitcast.22, f32[4,16,2176]{2,1,0:T(8,128)} %bitcast.21, f32[8,2048]{1,0:T(8,128)} %bitcast.24, ...), custom_call_target="tpu_custom_call" | custom-call | tf_op jit(solution)/shard_map/sweeps/pallas_call | solution.py:436
  121.5 0.7 slice_bitcast_fusion
  122.2 19.9 %psum.7 = f32[4]{0:T(128)S(1)} all-reduce(f32[4]{0:T(128)S(1)} %slice_bitcast_fusion), channel_id=1, replica_groups=mesh['sky'=8,'band'=4] {'sky'}, use_global_device_ids=true, to_apply=%region_3.4 | all-reduce | flops 4 | bytes 32 | tf_op jit(solution)/shard_map/psum | solution.py:394
  142.1 0.5 multiply_bitcast_fusion
  (1 shorter events, 0.0 us)
Async XLA Ops:
  7.2 82.6 %all-gather.4.cloned.1.call-start = ((), (), s32[]{:S(2)}) async-start(), calls=%async_computation | async-start | bytes 4460544 | tf_op jit(solution)/shard_map/all_gather | solution.py:390
Sparse Core Ops, SparseCore 0:
  26.8 62.8 all-gather.3
